TPU v7x, 32 devices: a whole 2x2x4 slice. The times are simulated.
32 devices in a mesh: groups: 2 (over y), mp: 2 (over x), expert: 4 (over z), dp: 2 (over core).
Axes of the slice: x: 2, y: 2, z: 4, core: 2. Of those that a mesh axis runs over, the one named last changes fastest.
Arguments:
- hidden_in: bfloat16 [1024, 4096], P(('groups', 'expert', 'dp'), 'mp'), parts along dimension 0, may hold values from -6 to 6
- norm_gain: bfloat16 [2, 4096], P(None, 'mp'), may hold values from 0.25 to 1.75
- expert_ids: int32 [2, 1024, 2], P(None, ('groups', 'expert', 'dp')), parts along dimension 1, may hold values from 0 to 3, all different within a row; in each aligned block of 64 rows (0 to 63, 64 to 127, ..., all dimensions but the last counted through in order) at most 64 rows name the same one
- gate_counts: int32 [2, 1024, 2], P(None, ('groups', 'expert', 'dp')), parts along dimension 1, may hold values from 8 to 15
- exit_layer: int32 [1024], P(('groups', 'expert', 'dp')), parts along dimension 0, may hold values from 1 to 2
- w_gate: bfloat16 [2, 4, 7168, 4096], P(None, 'expert', ('mp', 'dp')), may hold values from -0.09375 to 0.09375
- w_up: bfloat16 [2, 4, 7168, 4096], P(None, 'expert', ('mp', 'dp')), may hold values from -0.09375 to 0.09375
- w_down: bfloat16 [2, 4, 7168, 4096], P(None, 'expert', ('mp', 'dp')), may hold values from -0.0625 to 0.0625
Outputs:
- hidden_out: bfloat16 [1024, 4096], P(('groups', 'expert', 'dp'), 'mp'), parts along dimension 0
There are 2 independent parts, one for each index of `groups`. A program takes and returns all parts, laid end to end along the dimension named above; an argument that names none is the same for every part. Nothing has to cross between parts.
Inputs may be any that keep to these rules, and one draw needn't show every extreme that they name: `expert_ids`: A token's two ids in a layer differ. In the rows of one device in one layer (aligned blocks of 64 rows, layer by layer) some expert may be named by all 64 rows.
All inputs are finite; a program needn't handle non-finite values.
Results may differ from a plain program's by a relative error of at most 0.014.
Values may be sent and summed in bfloat16 or wider, within the bound.
A program may use at most 384 MiB of HBM per device.

v0:
```python
import functools

import jax
import jax.numpy as jnp
from jax import lax
from jax.experimental import pallas as pl
from jax.experimental.pallas import tpu as pltpu
from jax.sharding import PartitionSpec as P

LAYERS = 2


norm_floor = 0.1
MESH = pl.DeviceIdType.MESH
CHUNK = 16


def tile_of(length, best):
    tile = best
    while tile >= 128:
        if length % tile == 0:
            return tile
        tile //= 2
    return length


def layer_kernel(
    layer_idx, n, dp, mp,
    cur_ref, gain_ref, share_ref, wg_hbm, wu_hbm, wd_hbm, out_ref,
    wg, wu, wd, x, p, rd, rcw, rcc, xr, normed, hid, col, gains, shares,
    local_sem, w_sem, x_s, x_r, zcw_s, zcw_r, zcc_s, zcc_r, dp_s, dp_r,
    sd_s, sd_r, sz_s, sz_r, g_s, g_r, rd_s, rd_r, rcw_s, rcw_r, rcc_s, rcc_r, xr_s, xr_r,
):
    rows, width = cur_ref.shape
    full = width * mp
    units = wg.shape[0]
    pair = dp * rows
    e, m, d = lax.axis_index("expert"), lax.axis_index("mp"), lax.axis_index("dp")
    half = n // 2
    every = list(range(mp))

    def block(offset):
        return lax.rem(e + offset + n, n)

    def part(r):
        return lax.rem(m - r + mp, mp)

    def core(k):
        return lax.rem(d + k, dp)

    up_z, down_z = {"expert": block(1)}, {"expert": block(-1)}

    def remote(src, dst, ss, rs, dev):
        return pltpu.make_async_remote_copy(
            src_ref=src, dst_ref=dst, send_sem=ss, recv_sem=rs, device_id=dev, device_id_type=MESH
        )

    sent = []

    def send(copy):
        copy.start()
        sent.append(copy)

    weights = []
    for i, (src, dst) in enumerate(((wg_hbm, wg), (wu_hbm, wu), (wd_hbm, wd))):
        copy = pltpu.make_async_copy(src.at[layer_idx, 0], dst, w_sem.at[i])
        copy.start()
        weights.append(copy)
    mine = pltpu.make_async_copy(cur_ref, x.at[e, d, m], local_sem.at[0])
    mine.start()
    own_gain = pltpu.make_async_copy(gain_ref, gains.at[m], local_sem.at[1])
    own_gain.start()
    own_share = pltpu.make_async_copy(share_ref, shares.at[e, d], local_sem.at[2])
    own_share.start()

    barrier = pltpu.get_barrier_semaphore()
    peers = [{"mp": part(r)} for r in range(1, mp)] + [{"expert": block(k)} for k in range(1, n)]
    peers += [{"dp": core(k)} for k in range(1, dp)]
    for dev in peers:
        pl.semaphore_signal(barrier, inc=1, device_id=dev, device_id_type=MESH)
    pl.semaphore_wait(barrier, len(peers))
    mine.wait()
    own_gain.wait()
    own_share.wait()

    def piece(ref, j, going_up):
        if 2 * j == n:
            return ref.at[pl.ds(0 if going_up else rows // 2, rows // 2)]
        return ref

    def cw(j, blk):
        ref = piece(x.at[blk, d, m], j, True)
        return remote(ref, ref, zcw_s.at[j], zcw_r.at[j], up_z)

    def cc(j, blk):
        ref = piece(x.at[blk, d, m], j, False)
        return remote(ref, ref, zcc_s.at[j], zcc_r.at[j], down_z)

    def to_core(slot, r, blk):
        for k in range(1, dp):
            ref = x.at[blk, d, part(r)]
            send(remote(ref, ref, dp_s.at[slot, r, k], dp_r.at[slot, r, k], {"dp": core(k)}))

    def from_core(slot, blk):
        for k in range(1, dp):
            for r in every:
                ref = x.at[blk, core(dp - k), part(r)]
                remote(ref, ref, dp_s.at[slot, r, k], dp_r.at[slot, r, k],
                       {"dp": core(k)}).wait_recv()
            ref = shares.at[blk, core(dp - k)]
            remote(ref, ref, sd_s.at[slot, k], sd_r.at[slot, k], {"dp": core(k)}).wait_recv()

    def to_mp(slot, blk):
        for r in range(1, mp):
            ref = x.at[blk, d, m]
            send(remote(ref, ref, x_s.at[slot, r], x_r.at[slot, r], {"mp": lax.rem(m + r, mp)}))

    def from_mp(slot, blk):
        for r in range(1, mp):
            ref = x.at[blk, d, part(r)]
            remote(ref, ref, x_s.at[slot, r], x_r.at[slot, r],
                   {"mp": lax.rem(m + r, mp)}).wait_recv()
            to_core(slot, r, blk)

    def share_core(slot, blk):
        for k in range(1, dp):
            ref = shares.at[blk, d]
            send(remote(ref, ref, sd_s.at[slot, k], sd_r.at[slot, k], {"dp": core(k)}))

    def level_blocks(j):
        if j == 0:
            return [e]
        if 2 * j == n:
            return [block(j)]
        return [block(-j), block(j)]

    starts, slots, filled, slot = [], [], 0, 0
    for j in range(half + 1):
        starts.append(filled)
        slots.append(slot)
        count = 1 if j == 0 or 2 * j == n else 2
        filled += count * pair
        slot += count

    for r in range(1, mp):
        ref = gains.at[m]
        send(remote(ref, ref, g_s.at[r], g_r.at[r], {"mp": lax.rem(m + r, mp)}))
    for k in range(1, n):
        ref = shares.at[e, d]
        send(remote(ref, ref, sz_s.at[k], sz_r.at[k], {"expert": block(k)}))
    to_mp(0, e)
    send(cw(1, e))
    send(cc(1, e))
    share_core(0, e)
    to_core(0, 0, e)

    def arrive(j):
        blocks = level_blocks(j)
        low, high = slots[j], slots[j] + len(blocks) - 1
        cw(j, block(-j)).wait_recv()
        if j < half:
            send(cw(j + 1, block(-j)))
        if low != high:
            to_mp(low, block(-j))
            to_core(low, 0, block(-j))
        cc(j, block(j)).wait_recv()
        if j < half:
            send(cc(j + 1, block(j)))
        to_mp(high, block(j))
        to_core(high, 0, block(j))

    for r in range(1, mp):
        ref = gains.at[part(r)]
        remote(ref, ref, g_s.at[r], g_r.at[r], {"mp": lax.rem(m + r, mp)}).wait_recv()

    def shares_from(j):
        for i, blk in enumerate(level_blocks(j)):
            k = (j if i == 0 else n - j)
            ref = shares.at[blk, d]
            remote(ref, ref, sz_s.at[k], sz_r.at[k], {"expert": block(k)}).wait_recv()
            share_core(slots[j] + i, blk)

    def norm(place, blk):
        for c in range(dp):
            base = place * pair + c * rows
            lanes = lax.broadcasted_iota(jnp.int32, (rows, shares.shape[3]), 1)
            picked = jnp.where(lanes == e, shares[blk, c], 0.0)
            col[base:base + rows, :] = jnp.sum(picked, axis=1, keepdims=True)

            def chunk(i, _):
                at = pl.ds(pl.multiple_of(i * CHUNK, CHUNK), CHUNK)
                total = jnp.zeros((CHUNK, 1), jnp.float32)
                for q in every:
                    v = x[blk, c, q, at, :].astype(jnp.float32)
                    total = total + jnp.sum(v * v, axis=1, keepdims=True)
                inv = lax.rsqrt(total / full + norm_floor)
                to = pl.ds(pl.multiple_of(base + i * CHUNK, CHUNK), CHUNK)
                for q in every:
                    v = x[blk, c, q, at, :].astype(jnp.float32)
                    normed[to, q * width:(q + 1) * width] = (v * inv * gains[q]).astype(
                        jnp.bfloat16
                    )
                return 0

            lax.fori_loop(0, rows // CHUNK, chunk, 0)

    tile = tile_of(units, 256)
    contract = (((1,), (1,)), ((), ()))

    def hidden(start, blocks):
        for place, blk in enumerate(blocks):
            norm(place, blk)
        size = pair * len(blocks)

        def step(t, _):
            at = pl.ds(pl.multiple_of(t * tile, tile), tile)
            a = normed[0:size, :]
            g = lax.dot_general(a, wg[at, :], contract, preferred_element_type=jnp.float32)
            u = lax.dot_general(a, wu[at, :], contract, preferred_element_type=jnp.float32)
            h = g / (1.0 + jnp.exp(-g)) * u * col[0:size, :]
            hid[start:start + size, at] = h.astype(jnp.bfloat16)
            return 0

        if tile == units:
            a = normed[0:size, :]
            g = lax.dot_general(a, wg[...], contract, preferred_element_type=jnp.float32)
            u = lax.dot_general(a, wu[...], contract, preferred_element_type=jnp.float32)
            h = g / (1.0 + jnp.exp(-g)) * u * col[0:size, :]
            hid[start:start + size, :] = h.astype(jnp.bfloat16)
        else:
            lax.fori_loop(0, units // tile, step, 0)

    from_mp(0, e)
    arrive(1)
    from_core(0, e)
    weights[0].wait()
    weights[1].wait()
    hidden(0, [e])
    for j in range(1, half + 1):
        if j < half:
            arrive(j + 1)
        blocks = level_blocks(j)
        shares_from(j)
        for i, blk in enumerate(blocks):
            from_mp(slots[j] + i, blk)
        for i, blk in enumerate(blocks):
            from_core(slots[j] + i, blk)
        hidden(starts[j], blocks)

    weights[2].wait()
    ctile = tile_of(width, 256)

    def project(start, blocks):
        size = pair * len(blocks)
        for q in every:
            def step(t, _):
                at = pl.ds(pl.multiple_of(t * ctile, ctile), ctile)
                wide = pl.ds(pl.multiple_of(q * width + t * ctile, ctile), ctile)
                y = jnp.dot(hid[start:start + size, :], wd[:, wide],
                            preferred_element_type=jnp.float32).astype(jnp.bfloat16)
                for i, blk in enumerate(blocks):
                    for c in range(dp):
                        base = i * pair + c * rows
                        p[blk, c, q, :, at] = y[base:base + rows]
                return 0

            lax.fori_loop(0, width // ctile, step, 0)

    def add(blk, q, others, begin=0, count=rows):
        def chunk(i, _):
            at = pl.ds(pl.multiple_of(begin + i * CHUNK, CHUNK), CHUNK)
            v = p[blk, d, q, at, :].astype(jnp.float32)
            for ref, index in others:
                v = v + ref[index + (at, slice(None))].astype(jnp.float32)
            p[blk, d, q, at, :] = v.astype(jnp.bfloat16)
            return 0

        lax.fori_loop(0, count // CHUNK, chunk, 0)

    def back_cw(j, blk):
        return remote(piece(p.at[blk, d, m], j, True), piece(rcw.at[j - 1], j, True),
                      rcw_s.at[j], rcw_r.at[j], up_z)

    def back_cc(j, blk):
        return remote(piece(p.at[blk, d, m], j, False), piece(rcc.at[j - 1], j, False),
                      rcc_s.at[j], rcc_r.at[j], down_z)

    def swap(slot, k, blk):
        return remote(p.at[blk, core(k)], rd.at[slot, k - 1], rd_s.at[slot, k], rd_r.at[slot, k],
                      {"dp": core(k)})

    def back_mp(slot, r, blk):
        return remote(p.at[blk, d, part(r)], xr.at[slot, r - 1], xr_s.at[slot, r],
                      xr_r.at[slot, r], {"mp": part(r)})

    def across(j):
        blocks = level_blocks(j)
        project(starts[j], blocks)
        for i, blk in enumerate(blocks):
            for k in range(1, dp):
                send(swap(slots[j] + i, k, blk))
        for i, blk in enumerate(blocks):
            for k in range(1, dp):
                swap(slots[j] + i, k, blk).wait_recv()
            for r in range(1, mp):
                q = part(r)
                add(blk, q, [(rd, (slots[j] + i, k - 1, q)) for k in range(1, dp)])
                send(back_mp(slots[j] + i, r, blk))

    across(half)
    for j in range(half, -1, -1):
        if j > 0:
            across(j - 1)
        blocks = level_blocks(j)
        for i, blk in enumerate(blocks):
            upward = j > 0 and (len(blocks) == 1 or i == 1)
            downward = j > 0 and (len(blocks) == 1 or i == 0)
            others = [(rd, (slots[j] + i, k - 1, m)) for k in range(1, dp)]
            for r in range(1, mp):
                back_mp(slots[j] + i, r, blk).wait_recv()
                others.append((xr, (slots[j] + i, r - 1)))
            add(blk, m, others)
            if j < half and (upward or j == 0):
                back_cw(j + 1, blk).wait_recv()
                split = 2 * (j + 1) == n
                add(blk, m, [(rcw, (j,))], 0, rows // 2 if split else rows)
            if j < half and (downward or j == 0):
                back_cc(j + 1, blk).wait_recv()
                split = 2 * (j + 1) == n
                add(blk, m, [(rcc, (j,))], rows // 2 if split else 0,
                    rows // 2 if split else rows)
            if upward:
                send(back_cw(j, blk))
            if downward:
                send(back_cc(j, blk))

    def last(i, _):
        at = pl.ds(pl.multiple_of(i * CHUNK, CHUNK), CHUNK)
        v = p[e, d, m, at, :].astype(jnp.float32)
        out_ref[at, :] = (cur_ref[at, :].astype(jnp.float32) + v).astype(jnp.bfloat16)
        return 0

    lax.fori_loop(0, rows // CHUNK, last, 0)
    for copy in sent:
        copy.wait_send()


def layer(layer_idx, n, dp, mp, current, gain, share, w_gate, w_up, w_down):
    rows, width = current.shape
    units, full = w_gate.shape[2:]
    half = n // 2
    bf, dma = jnp.bfloat16, pltpu.SemaphoreType.DMA
    vmem = pl.BlockSpec(memory_space=pltpu.VMEM)
    hbm = pl.BlockSpec(memory_space=pl.ANY)
    return pl.pallas_call(
        functools.partial(layer_kernel, layer_idx, n, dp, mp),
        out_shape=jax.ShapeDtypeStruct((rows, width), bf),
        in_specs=[vmem, vmem, vmem, hbm, hbm, hbm],
        out_specs=vmem,
        scratch_shapes=[
            pltpu.VMEM((units, full), bf),
            pltpu.VMEM((units, full), bf),
            pltpu.VMEM((units, full), bf),
            pltpu.VMEM((n, dp, mp, rows, width), bf),
            pltpu.VMEM((n, dp, mp, rows, width), bf),
            pltpu.VMEM((n, max(dp - 1, 1), mp, rows, width), bf),
            pltpu.VMEM((half, rows, width), bf),
            pltpu.VMEM((half, rows, width), bf),
            pltpu.VMEM((n, max(mp - 1, 1), rows, width), bf),
            pltpu.VMEM((2 * dp * rows, full), bf),
            pltpu.VMEM((n * dp * rows, units), bf),
            pltpu.VMEM((2 * dp * rows, 1), jnp.float32),
            pltpu.VMEM((mp, 1, width), jnp.float32),
            pltpu.VMEM((n, dp, rows, share.shape[1]), jnp.float32),
            dma((3,)), dma((3,)), dma((n, mp)), dma((n, mp)),
            dma((half + 1,)), dma((half + 1,)), dma((half + 1,)), dma((half + 1,)),
            dma((n, mp, dp)), dma((n, mp, dp)),
            dma((n, dp)), dma((n, dp)), dma((n,)), dma((n,)), dma((mp,)), dma((mp,)),
            dma((n, dp)), dma((n, dp)),
            dma((half + 1,)), dma((half + 1,)), dma((half + 1,)), dma((half + 1,)),
            dma((n, mp)), dma((n, mp)),
        ],
        compiler_params=pltpu.CompilerParams(
            collective_id=layer_idx, has_side_effects=True, vmem_limit_bytes=67043328
        ),
    )(current, gain, share, w_gate, w_up, w_down)


def body(hidden_in, norm_gain, expert_ids, gate_counts, exit_layer, w_gate, w_up, w_down):
    n, dp, mp = lax.axis_size("expert"), lax.axis_size("dp"), lax.axis_size("mp")
    rows, width = hidden_in.shape
    expert_range = jnp.arange(n, dtype=jnp.int32)
    counts = gate_counts.astype(jnp.float32)
    gate_share = counts / jnp.sum(counts, axis=2, keepdims=True)
    active = exit_layer[None, :] > jnp.arange(LAYERS, dtype=jnp.int32)[:, None]
    matched = (expert_ids[..., None] == expert_range) & active[:, :, None, None]
    share = jnp.sum(jnp.where(matched, gate_share[..., None], jnp.float32(0.0)), axis=2)
    share = jnp.pad(share, ((0, 0), (0, 0), (0, -n % 128)))
    gain = norm_gain.astype(jnp.float32)[:, None, :]
    current = hidden_in
    for layer_idx in range(LAYERS):
        current = layer(
            layer_idx, n, dp, mp, current, gain[layer_idx], share[layer_idx], w_gate, w_up, w_down
        )
    return current


def solution(mesh):
    in_specs = (
        P(("groups", "expert", "dp"), "mp"),
        P(None, "mp"),
        P(None, ("groups", "expert", "dp"), None),
        P(None, ("groups", "expert", "dp"), None),
        P(("groups", "expert", "dp")),
        P(None, "expert", ("mp", "dp"), None),
        P(None, "expert", ("mp", "dp"), None),
        P(None, "expert", ("mp", "dp"), None),
    )
    out_specs = P(("groups", "expert", "dp"), "mp")
    return jax.shard_map(body, mesh=mesh, in_specs=in_specs, out_specs=out_specs, check_vma=False)
```

profile of v0, /device:TPU:0, one launch (start us, length us, event | category | flops | bytes accessed | tf_op | source)
XLA Modules:
  0.0 204.9 jit_solution(9136854364386584722)
XLA Ops:
  0.0 0.7 iota_compare_fusion.1
  0.7 0.8 convert_divide_fusion
  1.4 0.7 select_reduce_fusion
  2.1 1.4 fusion.8
  3.5 0.1 copy.11
  3.6 0.6 fusion.1
  4.3 101.1 %shard_map.82.cur_ref = bf16[64,2048]{1,0:T(8,128)(2,1)} custom-call(bf16[64,2048]{1,0:T(8,128)(2,1)} %cur_ref.1, f32[1,2048]{1,0:T(1,128)} %get-tuple-element.8.gain_ref, f32[64,128]{1,0:T(8,128)} %get-tuple-element.6.share_ref, bf16[2,1,1792,4096]{3,2,1,0:T(8,128)(2,1)} %wg_hbm.3, bf16[2,1,1792,4096]{3,2,1,0:T(8,128)(2,1)} %wu_hbm.3, ...), custom_call_target="tpu_custom_call" | custom-call | tf_op jit(solution)/shard_map/pallas_call | solution.py:355
  105.4 97.9 %shard_map.83 = bf16[64,2048]{1,0:T(8,128)(2,1)} custom-call(bf16[64,2048]{1,0:T(8,128)(2,1)} %shard_map.82.cur_ref, f32[1,2048]{1,0:T(1,128)} %get-tuple-element.7.gain_ref, f32[64,128]{1,0:T(8,128)} %get-tuple-element.5.share_ref, bf16[2,1,1792,4096]{3,2,1,0:T(8,128)(2,1)} %wg_hbm.3, bf16[2,1,1792,4096]{3,2,1,0:T(8,128)(2,1)} %wu_hbm.3, ...), custom_call_target="tpu_custom_call" | custom-call | tf_op jit(solution)/shard_map/pallas_call | solution.py:355
  203.3 1.7 copy.13
where the time goes:
time: 205 us
  Pallas kernels  199 us (97%)
  local copies, waits for them, and re-layouts  3.8 us (2%)
  other arithmetic  2.13 us (1%)
    pallas_call x2, Pallas kernels, layer(): pl.pallas_call(functools.partial(layer_kernel, layer_idx, n, dp, mp), out...  199 us

commit v1 on v0

v1 whole, which is shorter than its diff:
```python
import functools

import jax
import jax.numpy as jnp
from jax import lax
from jax.experimental import pallas as pl
from jax.experimental.pallas import tpu as pltpu
from jax.sharding import PartitionSpec as P

LAYERS = 2
HALVES = 2
PARTS = 2
LANES = 128

norm_floor = 0.1
MESH = pl.DeviceIdType.MESH
CHUNK = 16


def tile_of(length, best):
    tile = best
    while tile >= 128:
        if length % tile == 0:
            return tile
        tile //= 2
    return length


def stack_kernel(
    n, dp, mp,
    cur_ref, gain_ref, share_ref, wg_hbm, wu_hbm, wd_hbm, out_ref,
    wg, wu, wd, xg, p, rd, xr, rzu, rzd, hid, col, inv, shares,
    w_sem, sh_s, sh_r, zu_s, zu_r, zd_s, zd_r, x_s, x_r, d_s, d_r,
    sw_s, sw_r, bx_s, bx_r, bu_s, bu_r, bd_s, bd_r,
):
    rows, width = cur_ref.shape
    full = width * mp
    units = wg.shape[0]
    hr = rows // HALVES
    pr = hr // PARTS
    core_rows = n * hr
    size = dp * core_rows
    e, m, d = lax.axis_index("expert"), lax.axis_index("mp"), lax.axis_index("dp")
    tile = tile_of(units, 256)
    steps = units // tile
    ctile = tile_of(width, 1024)
    csteps = width // ctile
    contract = (((1,), (1,)), ((), ()))

    def part(r):
        return lax.rem(m - r + mp, mp)

    def ahead(r):
        return {"mp": lax.rem(m + r, mp)}

    def core(k):
        return lax.rem(d + k, dp)

    place_of = {k: e + k for k in range(1 - n, n)}
    has = {k: (e + k <= n - 1 if k > 0 else e + k >= 0) for k in range(1 - n, n) if k}
    below, above = e > 0, e < n - 1
    up_z, down_z = {"expert": lax.rem(e + 1, n)}, {"expert": lax.rem(e + n - 1, n)}

    def remote(src, dst, ss, rs, dev):
        return pltpu.make_async_remote_copy(
            src_ref=src, dst_ref=dst, send_sem=ss, recv_sem=rs, device_id=dev, device_id_type=MESH
        )

    def when(cond, run):
        if cond is None:
            run()
        else:
            pl.when(cond)(run)

    sent = {}

    def send(group, make, *conds):
        make().start()
        sent.setdefault(group, []).append((make, conds))

    def drain(group):
        for make, conds in sent.pop(group, []):
            cond = None
            for c in conds:
                cond = c if cond is None else jnp.logical_and(cond, c)
            when(cond, lambda make=make: make().wait_send())

    def weight(layer_idx, i):
        src, dst = ((wg_hbm, wg), (wu_hbm, wu), (wd_hbm, wd))[i]
        return pltpu.make_async_copy(src.at[layer_idx, 0], dst, w_sem.at[i])

    def row_of(c, blk, j=0):
        return pl.multiple_of((c * n + blk) * hr + j * pr, pr)

    def block_ref(h, blk, j, c, q):
        return xg.at[h, q, pl.ds(row_of(c, blk, j), pr)]

    def zu(h, s, j, blk):
        ref = block_ref(h, blk, j, d, m)
        return remote(ref, ref, zu_s.at[h, s, j], zu_r.at[h, s, j], up_z)

    def zd(h, s, j, blk):
        ref = block_ref(h, blk, j, d, m)
        return remote(ref, ref, zd_s.at[h, s, j], zd_r.at[h, s, j], down_z)

    def xm(h, blk, j, r, q):
        ref = block_ref(h, blk, j, d, q)
        return remote(ref, ref, x_s.at[h, blk, j, r], x_r.at[h, blk, j, r], ahead(r))

    def dc(h, blk, j, r, k, c):
        ref = block_ref(h, blk, j, c, part(r))
        return remote(ref, ref, d_s.at[h, blk, j, r, k], d_r.at[h, blk, j, r, k], {"dp": core(k)})

    def spread(h, j, blk, *conds):
        for r in range(1, mp):
            send(("gather", h), lambda r=r: xm(h, blk, j, r, m), *conds)
        to_core(h, blk, j, 0, *conds)

    def to_core(h, blk, j, r, *conds):
        for k in range(1, dp):
            send(("gather", h), lambda k=k: dc(h, blk, j, r, k, d), *conds)

    def own_z(h, j):
        pl.when(above)(lambda: send(("gather", h), lambda: zu(h, 1, j, e), above))
        pl.when(below)(lambda: send(("gather", h), lambda: zd(h, 1, j, e), below))

    def z_step(h, s, j):
        low, high = place_of[-s], place_of[s]

        def from_below():
            zu(h, s, j, low).wait_recv()
            if s + 1 < n:
                pl.when(above)(
                    lambda: send(("gather", h), lambda: zu(h, s + 1, j, low), has[-s], above)
                )
            spread(h, j, low, has[-s])

        def from_above():
            zd(h, s, j, high).wait_recv()
            if s + 1 < n:
                pl.when(below)(
                    lambda: send(("gather", h), lambda: zd(h, s + 1, j, high), has[s], below)
                )
            spread(h, j, high, has[s])

        pl.when(has[-s])(from_below)
        pl.when(has[s])(from_above)

    def x_step(h, s):
        def take(blk, *conds):
            for j in range(PARTS):
                for r in range(1, mp):
                    xm(h, blk, j, r, part(r)).wait_recv()
                    to_core(h, blk, j, r, *conds)

        if s == 0:
            take(e)
        else:
            pl.when(has[-s])(lambda: take(place_of[-s], has[-s]))
            pl.when(has[s])(lambda: take(place_of[s], has[s]))

    def core_done(h):
        for k in range(1, dp):
            for blk in range(n):
                for j in range(PARTS):
                    for r in range(mp):
                        dc(h, blk, j, r, k, core(dp - k)).wait_recv()

    def own_rows(h, layer_idx, current):
        gain = gain_ref[...].astype(jnp.float32)[layer_idx:layer_idx + 1, :]
        lanes = lax.broadcasted_iota(jnp.int32, (CHUNK, LANES), 1)

        def chunk(i, _):
            at = pl.ds(pl.multiple_of(h * hr + i * CHUNK, CHUNK), CHUNK)
            v = current[at, :].astype(jnp.float32)
            left = jnp.sum(v * v, axis=1, keepdims=True)
            tail = jnp.zeros((CHUNK, LANES), jnp.float32)
            for lane in range(3):
                held = left.astype(jnp.bfloat16).astype(jnp.float32)
                tail = jnp.where(lanes == lane, held, tail)
                left = left - held
            to = pl.ds(pl.multiple_of(row_of(d, e) + i * CHUNK, CHUNK), CHUNK)
            xg[h, m, to, 0:width] = (v * gain).astype(jnp.bfloat16)
            xg[h, m, to, width:width + LANES] = tail.astype(jnp.bfloat16)
            return 0

        lax.fori_loop(0, hr // CHUNK, chunk, 0)

    def scales(h, layer_idx):
        total = jnp.zeros((size, 1), jnp.float32)
        for q in range(mp):
            tail = xg[h, q, :, width:width + LANES].astype(jnp.float32)
            total = total + jnp.sum(tail, axis=1, keepdims=True)
        scale = lax.rsqrt(total / full + norm_floor)
        inv[0] = scale
        inv[1] = scale * col[layer_idx, h]

    def hidden(h, layer_idx, events):
        def step(t, _):
            at = pl.ds(pl.multiple_of(t * tile, tile), tile)
            g = u = None
            for q in range(mp):
                a = xg[h, q, :, 0:width]
                wide = slice(q * width, (q + 1) * width)
                gq = lax.dot_general(a, wg[at, wide], contract, preferred_element_type=jnp.float32)
                uq = lax.dot_general(a, wu[at, wide], contract, preferred_element_type=jnp.float32)
                g, u = (gq, uq) if q == 0 else (g + gq, u + uq)
            g = g * inv[0]
            y = g / (1.0 + jnp.exp(-g)) * (u * inv[1])
            hid[:, at] = y.astype(jnp.bfloat16)
            for place, run in events:
                if steps == 1:
                    run()
                else:
                    pl.when(t == min(place * steps // 7, steps - 1))(run)
            return 0

        if steps == 1:
            step(0, 0)
        else:
            lax.fori_loop(0, steps, step, 0)

    def project(h, first, count):
        def step(t, _):
            q = part(first + t // csteps)
            off = lax.rem(t, csteps) * ctile
            wide = pl.ds(pl.multiple_of(q * width + off, ctile), ctile)
            y = jnp.dot(hid[...], wd[:, wide], preferred_element_type=jnp.float32)
            p[h, q, :, pl.ds(pl.multiple_of(off, ctile), ctile)] = y.astype(jnp.bfloat16)
            return 0

        lax.fori_loop(0, count * csteps, step, 0)

    def swap(h, q, r, k):
        src = p.at[h, q, pl.ds(pl.multiple_of(core(k) * core_rows, core_rows), core_rows)]
        return remote(src, rd.at[h, k - 1, q], sw_s.at[h, r, k], sw_r.at[h, r, k], {"dp": core(k)})

    def swap_start(h, r):
        for k in range(1, dp):
            send(("home", h), lambda k=k: swap(h, part(r), r, k))

    def swap_wait(h, r):
        for k in range(1, dp):
            swap(h, part(r), r, k).wait_recv()

    def chunks(j, count, run):
        def chunk(i, _):
            run(pl.multiple_of(j * pr + i * CHUNK, CHUNK))
            return 0

        if count == CHUNK:
            chunk(0, 0)
        else:
            lax.fori_loop(0, count // CHUNK, chunk, 0)

    def with_cores(h, q, blk, off):
        at = pl.ds(pl.multiple_of(row_of(d, blk) + off, CHUNK), CHUNK)
        other = pl.ds(pl.multiple_of(blk * hr + off, CHUNK), CHUNK)
        v = p[h, q, at, :].astype(jnp.float32)
        for k in range(1, dp):
            v = v + rd[h, k - 1, q, other, :].astype(jnp.float32)
        return at, other, v

    def bx(h, blk, j, r):
        src = p.at[h, part(r), pl.ds(row_of(d, blk, j), pr)]
        dst = xr.at[h, r - 1, pl.ds(pl.multiple_of(blk * hr + j * pr, pr), pr)]
        return remote(src, dst, bx_s.at[h, blk, j, r], bx_r.at[h, blk, j, r], {"mp": part(r)})

    def by_distance(k, run):
        if k == 0:
            run(e)
        else:
            pl.when(has[k])(lambda: run(place_of[k], has[k]))
            pl.when(has[-k])(lambda: run(place_of[-k], has[-k]))

    def back_x(h, k):
        def run(blk, *conds):
            for j in range(PARTS):
                for r in range(1, mp):
                    def put(off, q=part(r)):
                        at, _, v = with_cores(h, q, blk, off)
                        p[h, q, at, :] = v.astype(jnp.bfloat16)

                    chunks(j, pr, put)
                    send(("home", h), lambda j=j, r=r: bx(h, blk, j, r), *conds)

        by_distance(k, run)

    def bu(h, blk, j):
        src = p.at[h, m, pl.ds(row_of(d, blk, j), pr)]
        return remote(src, rzu.at[h, blk, pl.ds(j * pr, pr)], bu_s.at[h, blk, j], bu_r.at[h, blk, j], up_z)

    def bd(h, blk, j):
        src = p.at[h, m, pl.ds(row_of(d, blk, j), pr)]
        return remote(src, rzd.at[h, blk, pl.ds(j * pr, pr)], bd_s.at[h, blk, j], bd_r.at[h, blk, j], down_z)

    def gathered(h, blk, off):
        at, other, v = with_cores(h, m, blk, off)
        for r in range(1, mp):
            v = v + xr[h, r - 1, other, :].astype(jnp.float32)
        return at, v

    def plain(h, blk, j):
        def put(off):
            at, v = gathered(h, blk, off)
            p[h, m, at, :] = v.astype(jnp.bfloat16)

        chunks(j, pr, put)

    def joined(h, blk, j, incoming):
        def put(off):
            at, v = gathered(h, blk, off)
            v = v + incoming[h, blk, pl.ds(off, CHUNK), :].astype(jnp.float32)
            p[h, m, at, :] = v.astype(jnp.bfloat16)

        chunks(j, pr, put)

    def back_z(h, k, j):
        def along(blk, cond, copy, inner, incoming):
            for r in range(1, mp):
                bx(h, blk, j, r).wait_recv()

            @pl.when(inner)
            def _():
                copy(h, blk, j).wait_recv()
                joined(h, blk, j, incoming)

            pl.when(jnp.logical_not(inner))(lambda: plain(h, blk, j))
            send(("home", h), lambda: copy(h, blk, j), cond)

        pl.when(has[k])(lambda: along(place_of[k], has[k], bu, below, rzu))
        pl.when(has[-k])(lambda: along(place_of[-k], has[-k], bd, above, rzd))

    def arrive(h, current):
        for j in range(PARTS):
            for r in range(1, mp):
                bx(h, e, j, r).wait_recv()
            pl.when(below)(lambda j=j: bu(h, e, j).wait_recv())
            pl.when(above)(lambda j=j: bd(h, e, j).wait_recv())

        def finish(sources):
            def put(off):
                _, v = gathered(h, e, off)
                for ref in sources:
                    v = v + ref[h, e, pl.ds(off, CHUNK), :].astype(jnp.float32)
                at = pl.ds(pl.multiple_of(h * hr + off, CHUNK), CHUNK)
                out_ref[at, :] = (current[at, :].astype(jnp.float32) + v).astype(jnp.bfloat16)

            chunks(0, hr, put)

        if n == 1:
            finish([])
        else:
            pl.when(jnp.logical_not(below))(lambda: finish([rzd]))
            pl.when(jnp.logical_not(above))(lambda: finish([rzu]))
            if n > 2:
                pl.when(jnp.logical_and(below, above))(lambda: finish([rzu, rzd]))

    slot = d * n + e
    shares[slot] = share_ref[...]
    own_rows(0, 0, cur_ref)
    barrier = pltpu.get_barrier_semaphore()
    others = [(k, c) for k in range(n) for c in range(dp) if k + c > 0]
    peers = [ahead(r) for r in range(1, mp)]
    peers += [{"expert": lax.rem(e + k, n), "dp": core(c)} for k, c in others]
    for dev in peers:
        pl.semaphore_signal(barrier, inc=1, device_id=dev, device_id_type=MESH)
    pl.semaphore_wait(barrier, len(peers))

    def share_copy(k, c, place):
        ref = shares.at[place]
        return remote(ref, ref, sh_s.at[k, c], sh_r.at[k, c],
                      {"expert": lax.rem(e + k, n), "dp": core(c)})

    def columns():
        for k, c in others:
            place = lax.rem(d - c + dp, dp) * n + lax.rem(e - k + n, n)
            share_copy(k, c, place).wait_recv()
        lanes = lax.broadcasted_iota(jnp.int32, (shares.shape[2], shares.shape[1]), 1)
        for place in range(n * dp):
            tokens = shares[place].T
            for layer_idx in range(LAYERS):
                picked = jnp.sum(
                    jnp.where(lanes == layer_idx * n + e, tokens, 0.0), axis=1, keepdims=True
                )
                for h in range(HALVES):
                    col[layer_idx, h, place * hr:(place + 1) * hr, :] = picked[h * hr:(h + 1) * hr]

    both = range(PARTS)
    far = list(range(n - 1, 0, -1))

    def start_own(h):
        for j in both:
            own_z(h, j)
            spread(h, j, e)

    def z_all(h, s):
        for j in both:
            z_step(h, s, j)

    def back_all(h, k):
        for j in both:
            back_z(h, k, j)

    for layer_idx in range(LAYERS):
        if layer_idx == 0:
            start_own(0)
            for k, c in others:
                send(("share", 0), lambda k=k, c=c: share_copy(k, c, slot))
            for i in range(3):
                weight(0, i).start()
            own_rows(1, 0, cur_ref)
            columns()
            for s in range(1, n):
                z_all(0, s)
                if s == n - 2:
                    start_own(1)
            if n < 3:
                start_own(1)
        else:
            arrive(0, cur_ref)
            own_rows(0, layer_idx, out_ref)
            start_own(0)
            for k in far:
                back_all(1, k)
                z_all(0, n - k)
            arrive(1, cur_ref)
            own_rows(1, layer_idx, out_ref)
            start_own(1)
        for s in range(n - 1):
            x_step(0, s)
        if n > 1:
            z_all(1, 1)
        x_step(0, n - 1)
        core_done(0)
        scales(0, layer_idx)
        weight(layer_idx, 0).wait()
        weight(layer_idx, 1).wait()
        events = [(2 * s - 4, lambda s=s: z_all(1, s)) for s in range(2, n)]
        events += [(2 + s, lambda s=s: x_step(1, s)) for s in range(n - 1)]
        hidden(0, layer_idx, events)
        weight(layer_idx, 2).wait()
        drain(("home", 0))
        drain(("gather", 0))
        project(0, 1, mp - 1)
        for r in range(1, mp):
            swap_start(0, r)
        x_step(1, n - 1)
        project(0, 0, 1)
        swap_start(0, 0)
        for r in range(1, mp):
            swap_wait(0, r)
        for k in far + [0]:
            back_x(0, k)
        swap_wait(0, 0)
        core_done(1)
        scales(1, layer_idx)
        rest = [(k, j) for k in far for j in both]
        late = rest[-1:]
        spots = [1, 2, 4, 5, 6]
        events = [
            (spots[min(i, 4)], lambda k=k, j=j: back_z(0, k, j)) for i, (k, j) in enumerate(rest[:-1])
        ]
        hidden(1, layer_idx, events)
        if layer_idx + 1 < LAYERS:
            weight(layer_idx + 1, 0).start()
            weight(layer_idx + 1, 1).start()
        drain(("home", 1))
        drain(("gather", 1))
        project(1, 1, mp - 1)
        for r in range(1, mp):
            swap_start(1, r)
        for k, j in late:
            back_z(0, k, j)
        project(1, 0, 1)
        swap_start(1, 0)
        if layer_idx + 1 < LAYERS:
            weight(layer_idx + 1, 2).start()
        for r in range(1, mp):
            swap_wait(1, r)
        for k in far + [0]:
            back_x(1, k)
        swap_wait(1, 0)
    arrive(0, out_ref)
    for k in far:
        back_all(1, k)
    arrive(1, out_ref)
    for group in list(sent):
        drain(group)


def stack(n, dp, mp, current, gain, share, w_gate, w_up, w_down):
    rows, width = current.shape
    units, full = w_gate.shape[2:]
    hr = rows // HALVES
    size = n * dp * hr
    bf, f32, dma = jnp.bfloat16, jnp.float32, pltpu.SemaphoreType.DMA
    vmem = pl.BlockSpec(memory_space=pltpu.VMEM)
    hbm = pl.BlockSpec(memory_space=pl.ANY)

    def pair(*shape):
        return [dma(shape), dma(shape)]

    return pl.pallas_call(
        functools.partial(stack_kernel, n, dp, mp),
        out_shape=jax.ShapeDtypeStruct((rows, width), bf),
        in_specs=[vmem, vmem, vmem, hbm, hbm, hbm],
        out_specs=vmem,
        scratch_shapes=[
            pltpu.VMEM((units, full), bf),
            pltpu.VMEM((units, full), bf),
            pltpu.VMEM((units, full), bf),
            pltpu.VMEM((HALVES, mp, size, width + LANES), bf),
            pltpu.VMEM((HALVES, mp, size, width), bf),
            pltpu.VMEM((HALVES, max(dp - 1, 1), mp, n * hr, width), bf),
            pltpu.VMEM((HALVES, max(mp - 1, 1), n * hr, width), bf),
            pltpu.VMEM((HALVES, n, hr, width), bf),
            pltpu.VMEM((HALVES, n, hr, width), bf),
            pltpu.VMEM((size, units), bf),
            pltpu.VMEM((LAYERS, HALVES, size, 1), f32),
            pltpu.VMEM((2, size, 1), f32),
            pltpu.VMEM((n * dp,) + share.shape, f32),
            dma((3,)),
            *pair(n, dp), *pair(HALVES, n, PARTS), *pair(HALVES, n, PARTS),
            *pair(HALVES, n, PARTS, mp), *pair(HALVES, n, PARTS, mp, dp),
            *pair(HALVES, mp, dp), *pair(HALVES, n, PARTS, mp),
            *pair(HALVES, n, PARTS), *pair(HALVES, n, PARTS),
        ],
        compiler_params=pltpu.CompilerParams(
            collective_id=0, has_side_effects=True, vmem_limit_bytes=67043328
        ),
    )(current, gain, share, w_gate, w_up, w_down)


def body(hidden_in, norm_gain, expert_ids, gate_counts, exit_layer, w_gate, w_up, w_down):
    n, dp, mp = lax.axis_size("expert"), lax.axis_size("dp"), lax.axis_size("mp")
    rows = hidden_in.shape[0]
    expert_range = jnp.arange(n, dtype=jnp.int32)
    counts = gate_counts.astype(jnp.float32)
    gate_share = counts / jnp.sum(counts, axis=2, keepdims=True)
    active = exit_layer[None, :] > jnp.arange(LAYERS, dtype=jnp.int32)[:, None]
    matched = (expert_ids[..., None] == expert_range) & active[:, :, None, None]
    share = jnp.sum(jnp.where(matched, gate_share[..., None], jnp.float32(0.0)), axis=2)
    share = share.transpose(0, 2, 1).reshape(LAYERS * n, rows)
    share = jnp.pad(share, ((0, -(LAYERS * n) % 8), (0, -rows % 128)))
    return stack(n, dp, mp, hidden_in, norm_gain, share, w_gate, w_up, w_down)


def solution(mesh):
    in_specs = (
        P(("groups", "expert", "dp"), "mp"),
        P(None, "mp"),
        P(None, ("groups", "expert", "dp"), None),
        P(None, ("groups", "expert", "dp"), None),
        P(("groups", "expert", "dp")),
        P(None, "expert", ("mp", "dp"), None),
        P(None, "expert", ("mp", "dp"), None),
        P(None, "expert", ("mp", "dp"), None),
    )
    out_specs = P(("groups", "expert", "dp"), "mp")
    return jax.shard_map(body, mesh=mesh, in_specs=in_specs, out_specs=out_specs, check_vma=False)
```

time: 205 us -> 146 us (0.71)
  Pallas kernels: 199 us -> 141 us
    pallas_call x2 -> x1, Pallas kernels: 199 us -> 141 us  [stack(): pl.pallas_call(functools.partial(stack_kernel, n, dp, mp), out_shape=jax....]
where the time goes in v1:
time: 146 us
  Pallas kernels  141 us (97%)
  local copies, waits for them, and re-layouts  2.27 us (2%)
  other arithmetic  2.13 us (1%)
    pallas_call x1, Pallas kernels, stack(): pl.pallas_call(functools.partial(stack_kernel, n, dp, mp), out_shape=jax....  141 us

profile of v1, /device:TPU:0, one launch (start us, length us, event | category | flops | bytes accessed | tf_op | source)
XLA Modules:
  0.0 145.6 jit_solution(2380913849985872152)
XLA Ops:
  0.0 0.7 iota_compare_fusion.1
  0.7 0.8 convert_divide_fusion
  1.4 0.7 select_reduce_fusion
  2.1 0.6 pad.4.share_ref
  2.7 141.1 %shard_map.82 = bf16[64,2048]{1,0:T(8,128)(2,1)} custom-call(bf16[64,2048]{1,0:T(8,128)(2,1)} %cur_ref.1, bf16[2,2048]{1,0:T(2,128)(2,1)} %gain_ref.1, f32[8,128]{1,0:T(8,128)} %pad.4.share_ref, bf16[2,1,1792,4096]{3,2,1,0:T(8,128)(2,1)} %wg_hbm.1, bf16[2,1,1792,4096]{3,2,1,0:T(8,128)(2,1)} %wu_hbm.1, bf16[2,1,1792,4096]{3,2,1,0:T(8,128)(2,1)} %wd_hbm.1), custom_call_target="tpu_custom_call" | custom-call | tf_op jit(solution)/shard_map/pallas_call | solution.py:504
  143.9 1.7 %copy.12 = bf16[64,2048]{1,0:T(8,128)(2,1)} copy(bf16[64,2048]{1,0:T(8,128)(2,1)} %shard_map.82) | data formatting | bytes 524288

commit v2 on v1

v2 whole, which is shorter than its diff:
```python
import functools

import jax
import jax.numpy as jnp
from jax import lax
from jax.experimental import pallas as pl
from jax.experimental.pallas import tpu as pltpu
from jax.sharding import PartitionSpec as P

LAYERS = 2
HALVES = 2
PARTS = 2
LANES = 128

norm_floor = 0.1
MESH = pl.DeviceIdType.MESH
CHUNK = 16


def tile_of(length, best):
    tile = best
    while tile >= 128:
        if length % tile == 0:
            return tile
        tile //= 2
    return length


def stack_kernel(
    n, dp, mp,
    cur_ref, gain_ref, ids_ref, counts_ref, exit_ref, wg_hbm, wu_hbm, wd_hbm, out_ref,
    wg, wu, wd, xg, p, rd, xr, rzu, rzd, hid, col, inv, shares,
    w_sem, sh_s, sh_r, zu_s, zu_r, zd_s, zd_r, x_s, x_r, d_s, d_r,
    sw_s, sw_r, bx_s, bx_r, bu_s, bu_r, bd_s, bd_r,
):
    rows, width = cur_ref.shape
    full = width * mp
    units = wg.shape[0]
    hr = rows // HALVES
    pr = hr // PARTS
    core_rows = n * hr
    size = dp * core_rows
    e, m, d = lax.axis_index("expert"), lax.axis_index("mp"), lax.axis_index("dp")
    tile = tile_of(units, 256)
    steps = units // tile
    ctile = tile_of(width, 1024)
    csteps = width // ctile
    contract = (((1,), (1,)), ((), ()))

    def part(r):
        return lax.rem(m - r + mp, mp)

    def ahead(r):
        return {"mp": lax.rem(m + r, mp)}

    def core(k):
        return lax.rem(d + k, dp)

    place_of = {k: e + k for k in range(1 - n, n)}
    has = {k: (e + k <= n - 1 if k > 0 else e + k >= 0) for k in range(1 - n, n) if k}
    below, above = e > 0, e < n - 1
    up_z, down_z = {"expert": lax.rem(e + 1, n)}, {"expert": lax.rem(e + n - 1, n)}

    def remote(src, dst, ss, rs, dev):
        return pltpu.make_async_remote_copy(
            src_ref=src, dst_ref=dst, send_sem=ss, recv_sem=rs, device_id=dev, device_id_type=MESH
        )

    def weight(layer_idx, i):
        src, dst = ((wg_hbm, wg), (wu_hbm, wu), (wd_hbm, wd))[i]
        return pltpu.make_async_copy(src.at[layer_idx, 0], dst, w_sem.at[i])

    def row_of(c, blk, j=0):
        return pl.multiple_of((c * n + blk) * hr + j * pr, pr)

    def block_ref(h, blk, j, c, q):
        return xg.at[h, q, pl.ds(row_of(c, blk, j), pr)]

    def zu(h, s, j, blk):
        ref = block_ref(h, blk, j, d, m)
        return remote(ref, ref, zu_s.at[h], zu_r.at[h, s - 1, j], up_z)

    def zd(h, s, j, blk):
        ref = block_ref(h, blk, j, d, m)
        return remote(ref, ref, zd_s.at[h], zd_r.at[h, s - 1, j], down_z)

    def xm(h, blk, r, ref):
        return remote(ref, ref, x_s.at[h, r - 1], x_r.at[h, blk, r - 1], ahead(r))

    def dc(h, k, ref):
        return remote(ref, ref, d_s.at[h, k - 1], d_r.at[h, k - 1], {"dp": core(k)})

    def core_ref(h, c, q, first=0, count=n):
        at = pl.ds(pl.multiple_of(c * core_rows + first * hr, hr), count * hr)
        return xg.at[h, :, at] if q is None else xg.at[h, q, at]

    def spread(h, j, blk):
        for r in range(1, mp):
            xm(h, blk, r, block_ref(h, blk, j, d, m)).start()
        to_core(h, block_ref(h, blk, j, d, m))

    def to_core(h, ref):
        for k in range(1, dp):
            dc(h, k, ref).start()

    def own_z(h, j):
        pl.when(above)(lambda: zu(h, 1, j, e).start())
        pl.when(below)(lambda: zd(h, 1, j, e).start())

    def z_step(h, s, j):
        low, high = place_of[-s], place_of[s]

        def from_below():
            zu(h, s, j, low).wait_recv()
            if s + 1 < n:
                pl.when(above)(lambda: zu(h, s + 1, j, low).start())
            spread(h, j, low)

        def from_above():
            zd(h, s, j, high).wait_recv()
            if s + 1 < n:
                pl.when(below)(lambda: zd(h, s + 1, j, high).start())
            spread(h, j, high)

        pl.when(has[-s])(from_below)
        pl.when(has[s])(from_above)

    def x_step(h, s):
        def take(blk):
            for r in range(1, mp):
                ref = xg.at[h, part(r), pl.ds(row_of(d, blk), hr)]
                xm(h, blk, r, ref).wait_recv()
                to_core(h, ref)

        if s == 0:
            take(e)
        else:
            pl.when(has[-s])(lambda: take(place_of[-s]))
            pl.when(has[s])(lambda: take(place_of[s]))

    def core_done(h):
        for k in range(1, dp):
            dc(h, k, core_ref(h, core(dp - k), None)).wait_recv()

    def gather_sent(h):
        for k in range(1, dp):
            dc(h, k, core_ref(h, d, None)).wait_send()
        for r in range(1, mp):
            xm(h, e, r, core_ref(h, d, m)).wait_send()
        for i in range(n):
            def done(i=i):
                if i < n - 1:
                    ref = core_ref(h, d, m, 0, i + 1)
                    remote(ref, ref, zu_s.at[h], zu_r.at[h, 0, 0], up_z).wait_send()
                if i > 0:
                    ref = core_ref(h, d, m, i, n - i)
                    remote(ref, ref, zd_s.at[h], zd_r.at[h, 0, 0], down_z).wait_send()

            pl.when(e == i)(done)

    def own_rows(h, layer_idx, current):
        gain = gain_ref[...].astype(jnp.float32)[layer_idx:layer_idx + 1, :]
        lanes = lax.broadcasted_iota(jnp.int32, (CHUNK, LANES), 1)

        def chunk(i, _):
            at = pl.ds(pl.multiple_of(h * hr + i * CHUNK, CHUNK), CHUNK)
            v = current[at, :].astype(jnp.float32)
            left = jnp.sum(v * v, axis=1, keepdims=True)
            tail = jnp.zeros((CHUNK, LANES), jnp.float32)
            for lane in range(3):
                held = left.astype(jnp.bfloat16).astype(jnp.float32)
                tail = jnp.where(lanes == lane, held, tail)
                left = left - held
            to = pl.ds(pl.multiple_of(row_of(d, e) + i * CHUNK, CHUNK), CHUNK)
            xg[h, m, to, 0:width] = (v * gain).astype(jnp.bfloat16)
            xg[h, m, to, width:width + LANES] = tail.astype(jnp.bfloat16)
            return 0

        lax.fori_loop(0, hr // CHUNK, chunk, 0)

    def scales(h, layer_idx):
        total = jnp.zeros((size, 1), jnp.float32)
        for q in range(mp):
            tail = xg[h, q, :, width:width + LANES].astype(jnp.float32)
            total = total + jnp.sum(tail, axis=1, keepdims=True)
        scale = lax.rsqrt(total / full + norm_floor)
        inv[0] = scale
        inv[1] = scale * col[layer_idx, h]

    def hidden(h, layer_idx, events):
        def step(t, _):
            at = pl.ds(pl.multiple_of(t * tile, tile), tile)
            g = u = None
            for q in range(mp):
                a = xg[h, q, :, 0:width]
                wide = slice(q * width, (q + 1) * width)
                gq = lax.dot_general(a, wg[at, wide], contract, preferred_element_type=jnp.float32)
                uq = lax.dot_general(a, wu[at, wide], contract, preferred_element_type=jnp.float32)
                g, u = (gq, uq) if q == 0 else (g + gq, u + uq)
            g = g * inv[0]
            y = g / (1.0 + jnp.exp(-g)) * (u * inv[1])
            hid[:, at] = y.astype(jnp.bfloat16)
            for place, run in events:
                if steps == 1:
                    run()
                else:
                    pl.when(t == min(place * steps // 7, steps - 1))(run)
            return 0

        if steps == 1:
            step(0, 0)
        else:
            lax.fori_loop(0, steps, step, 0)

    def project(h, r, events=()):
        def step(t, _):
            q = part(r)
            off = pl.multiple_of(t * ctile, ctile)
            wide = pl.ds(pl.multiple_of(q * width + t * ctile, ctile), ctile)
            y = jnp.dot(hid[...], wd[:, wide], preferred_element_type=jnp.float32)
            p[h, q, :, pl.ds(off, ctile)] = y.astype(jnp.bfloat16)
            for k in range(1, dp):
                swap(h, r, k, pl.ds(off, ctile)).start()
            for place, run in events:
                pl.when(t == min(place, csteps - 1))(run)
            return 0

        lax.fori_loop(0, csteps, step, 0)

    def swap(h, r, k, at=None):
        q = part(r)
        rows_at = pl.ds(pl.multiple_of(core(k) * core_rows, core_rows), core_rows)
        src, dst = p.at[h, q, rows_at], rd.at[h, k - 1, q]
        if at is not None:
            src, dst = p.at[h, q, rows_at, at], rd.at[h, k - 1, q, :, at]
        return remote(src, dst, sw_s.at[h, r, k - 1], sw_r.at[h, r, k - 1], {"dp": core(k)})

    def swap_wait(h, r):
        for k in range(1, dp):
            swap(h, r, k).wait_recv()

    def chunks(j, count, run):
        def chunk(i, _):
            run(pl.multiple_of(j * pr + i * CHUNK, CHUNK))
            return 0

        if count == CHUNK:
            chunk(0, 0)
        else:
            lax.fori_loop(0, count // CHUNK, chunk, 0)

    def with_cores(h, q, blk, off):
        at = pl.ds(pl.multiple_of(row_of(d, blk) + off, CHUNK), CHUNK)
        other = pl.ds(pl.multiple_of(blk * hr + off, CHUNK), CHUNK)
        v = p[h, q, at, :].astype(jnp.float32)
        for k in range(1, dp):
            v = v + rd[h, k - 1, q, other, :].astype(jnp.float32)
        return at, other, v

    def bx(h, blk, j, r):
        src = p.at[h, part(r), pl.ds(row_of(d, blk, j), pr)]
        dst = xr.at[h, r - 1, pl.ds(pl.multiple_of(blk * hr + j * pr, pr), pr)]
        return remote(src, dst, bx_s.at[h, r - 1], bx_r.at[h, blk, j, r - 1], {"mp": part(r)})

    def by_distance(k, run):
        if k == 0:
            run(e)
        else:
            pl.when(has[k])(lambda: run(place_of[k]))
            pl.when(has[-k])(lambda: run(place_of[-k]))

    def back_x(h, k):
        def run(blk):
            for j in range(PARTS):
                for r in range(1, mp):
                    def put(off, q=part(r)):
                        at, _, v = with_cores(h, q, blk, off)
                        p[h, q, at, :] = v.astype(jnp.bfloat16)

                    chunks(j, pr, put)
                    bx(h, blk, j, r).start()

        by_distance(k, run)

    def bu(h, blk, j):
        src = p.at[h, m, pl.ds(row_of(d, blk, j), pr)]
        dst = rzu.at[h, blk, pl.ds(j * pr, pr)]
        return remote(src, dst, bu_s.at[h], bu_r.at[h, blk - 1, j], up_z)

    def bd(h, blk, j):
        src = p.at[h, m, pl.ds(row_of(d, blk, j), pr)]
        dst = rzd.at[h, blk, pl.ds(j * pr, pr)]
        return remote(src, dst, bd_s.at[h], bd_r.at[h, blk, j], down_z)

    def out_ref_of(h, q, first=0, count=n):
        return p.at[h, q, pl.ds(pl.multiple_of(d * core_rows + first * hr, hr), count * hr)]

    def home_sent(h):
        for r in range(mp):
            for k in range(1, dp):
                swap(h, r, k).wait_send()
        for r in range(1, mp):
            ref = out_ref_of(h, part(r))
            remote(ref, ref, bx_s.at[h, r - 1], bx_r.at[h, 0, 0, r - 1], {"mp": part(r)}).wait_send()
        for i in range(n):
            def done(i=i):
                if i < n - 1:
                    ref = out_ref_of(h, m, i + 1, n - 1 - i)
                    remote(ref, ref, bu_s.at[h], bu_r.at[h, 0, 0], up_z).wait_send()
                if i > 0:
                    ref = out_ref_of(h, m, 0, i)
                    remote(ref, ref, bd_s.at[h], bd_r.at[h, 0, 0], down_z).wait_send()

            pl.when(e == i)(done)

    def gathered(h, blk, off):
        at, other, v = with_cores(h, m, blk, off)
        for r in range(1, mp):
            v = v + xr[h, r - 1, other, :].astype(jnp.float32)
        return at, v

    def plain(h, blk, j):
        def put(off):
            at, v = gathered(h, blk, off)
            p[h, m, at, :] = v.astype(jnp.bfloat16)

        chunks(j, pr, put)

    def joined(h, blk, j, incoming):
        def put(off):
            at, v = gathered(h, blk, off)
            v = v + incoming[h, blk, pl.ds(off, CHUNK), :].astype(jnp.float32)
            p[h, m, at, :] = v.astype(jnp.bfloat16)

        chunks(j, pr, put)

    def back_z(h, k, j):
        def along(blk, copy, inner, incoming):
            for r in range(1, mp):
                bx(h, blk, j, r).wait_recv()

            @pl.when(inner)
            def _():
                copy(h, blk, j).wait_recv()
                joined(h, blk, j, incoming)

            pl.when(jnp.logical_not(inner))(lambda: plain(h, blk, j))
            copy(h, blk, j).start()

        pl.when(has[k])(lambda: along(place_of[k], bu, below, rzu))
        pl.when(has[-k])(lambda: along(place_of[-k], bd, above, rzd))

    def arrive(h, current):
        for j in range(PARTS):
            for r in range(1, mp):
                bx(h, e, j, r).wait_recv()
            pl.when(below)(lambda j=j: bu(h, e, j).wait_recv())
            pl.when(above)(lambda j=j: bd(h, e, j).wait_recv())

        def finish(sources):
            def put(off):
                _, v = gathered(h, e, off)
                for ref in sources:
                    v = v + ref[h, e, pl.ds(off, CHUNK), :].astype(jnp.float32)
                at = pl.ds(pl.multiple_of(h * hr + off, CHUNK), CHUNK)
                out_ref[at, :] = (current[at, :].astype(jnp.float32) + v).astype(jnp.bfloat16)

            chunks(0, hr, put)

        if n == 1:
            finish([])
        else:
            pl.when(jnp.logical_not(below))(lambda: finish([rzd]))
            pl.when(jnp.logical_not(above))(lambda: finish([rzu]))
            if n > 2:
                pl.when(jnp.logical_and(below, above))(lambda: finish([rzu, rzd]))

    slot = d * n + e
    others = [(k, c) for k in range(n) for c in range(dp) if k + c > 0]

    def share_copies():
        ref = shares.at[slot]
        return [remote(ref, ref, sh_s.at[0], sh_r.at[0],
                       {"expert": lax.rem(e + k, n), "dp": core(c)}) for k, c in others]

    def own_shares():
        tall = shares.shape[1]
        line = lax.broadcasted_iota(jnp.int32, (tall, rows), 0)
        tile = jnp.zeros((tall, rows), jnp.float32)
        for layer_idx in range(LAYERS):
            count = counts_ref[layer_idx].astype(jnp.float32)
            named = ids_ref[layer_idx] + layer_idx * n
            whole = jnp.sum(count, axis=0, keepdims=True)
            part_of = jnp.where(exit_ref[...] > layer_idx, count / whole, 0.0)
            for choice in range(count.shape[0]):
                hit = line == named[choice:choice + 1]
                tile = tile + jnp.where(hit, part_of[choice:choice + 1], 0.0)
        shares[slot] = jnp.zeros(shares.shape[1:], jnp.float32)
        shares[slot, :, 0:rows] = tile

    def columns():
        ref = shares.at[pl.ds(0, len(others))]
        if others:
            remote(ref, ref, sh_s.at[0], sh_r.at[0], {"expert": e}).wait_recv()
        lanes = lax.broadcasted_iota(jnp.int32, (shares.shape[2], shares.shape[1]), 1)
        for place in range(n * dp):
            tokens = shares[place].T
            for layer_idx in range(LAYERS):
                picked = jnp.sum(
                    jnp.where(lanes == layer_idx * n + e, tokens, 0.0), axis=1, keepdims=True
                )
                for h in range(HALVES):
                    col[layer_idx, h, place * hr:(place + 1) * hr, :] = picked[h * hr:(h + 1) * hr]

    barrier = pltpu.get_barrier_semaphore()
    peers = [ahead(r) for r in range(1, mp)]
    peers += [{"expert": lax.rem(e + k, n), "dp": core(c)} for k, c in others]
    for dev in peers:
        pl.semaphore_signal(barrier, inc=1, device_id=dev, device_id_type=MESH)
    own_rows(0, 0, cur_ref)
    own_shares()
    pl.semaphore_wait(barrier, len(peers))

    both = range(PARTS)
    far = list(range(n - 1, 0, -1))

    def start_own(h):
        for j in both:
            own_z(h, j)
            spread(h, j, e)

    def z_all(h, s):
        for j in both:
            z_step(h, s, j)

    def back_all(h, k):
        for j in both:
            back_z(h, k, j)

    def back_x_all(h):
        for r in range(1, mp):
            swap_wait(h, r)
        for k in far + [0]:
            back_x(h, k)

    for layer_idx in range(LAYERS):
        if layer_idx == 0:
            start_own(0)
            for copy in share_copies():
                copy.start()
            own_rows(1, 0, cur_ref)
            for j in both:
                spread(1, j, e)
            for s in range(1, n):
                z_all(0, s)
                if s == 1:
                    for i in range(3):
                        weight(0, i).start()
                if s == max(n - 2, 1):
                    for j in both:
                        own_z(1, j)
            columns()
        else:
            arrive(0, cur_ref)
            own_rows(0, layer_idx, out_ref)
            start_own(0)
            swap_wait(1, 0)
            for k in far:
                back_all(1, k)
                z_all(0, n - k)
            arrive(1, cur_ref)
            own_rows(1, layer_idx, out_ref)
            start_own(1)
        for s in range(n - 1):
            x_step(0, s)
        if n > 1:
            z_all(1, 1)
        x_step(0, n - 1)
        core_done(0)
        scales(0, layer_idx)
        weight(layer_idx, 0).wait()
        weight(layer_idx, 1).wait()
        events = [(2 * s - 2, lambda s=s: z_all(1, s)) for s in range(2, n)]
        events += [(5, lambda s=s: x_step(1, s)) for s in range(n - 2)]
        hidden(0, layer_idx, events)
        weight(layer_idx, 2).wait()
        if layer_idx > 0:
            home_sent(0)
        gather_sent(0)
        for r in range(1, mp):
            project(0, r)
        if n > 1:
            x_step(1, n - 2)
        project(0, 0, [(0, lambda: back_x_all(0))])
        x_step(1, n - 1)
        core_done(1)
        scales(1, layer_idx)
        rest = [(k, j) for k in far for j in both]
        late = rest[-1:]
        spots = [0, 1, 3, 4, 6]
        events = [(0, lambda: swap_wait(0, 0))]
        events += [
            (spots[min(i, 4)], lambda k=k, j=j: back_z(0, k, j)) for i, (k, j) in enumerate(rest[:-1])
        ]
        hidden(1, layer_idx, events)
        if layer_idx + 1 < LAYERS:
            weight(layer_idx + 1, 0).start()
            weight(layer_idx + 1, 1).start()
        if layer_idx > 0:
            home_sent(1)
        gather_sent(1)
        for r in range(1, mp):
            project(1, r)
        for k, j in late:
            back_z(0, k, j)
        project(1, 0, [(0, lambda: back_x_all(1))])
        if layer_idx + 1 < LAYERS:
            weight(layer_idx + 1, 2).start()
    arrive(0, out_ref)
    swap_wait(1, 0)
    for k in far:
        back_all(1, k)
    arrive(1, out_ref)
    for h in range(HALVES):
        home_sent(h)
    if others:
        ref = shares.at[pl.ds(0, len(others))]
        remote(ref, ref, sh_s.at[0], sh_r.at[0], {"expert": e}).wait_send()


def stack(n, dp, mp, current, gain, ids, counts, exits, w_gate, w_up, w_down):
    rows, width = current.shape
    units, full = w_gate.shape[2:]
    hr = rows // HALVES
    size = n * dp * hr
    bf, f32, dma = jnp.bfloat16, jnp.float32, pltpu.SemaphoreType.DMA
    vmem = pl.BlockSpec(memory_space=pltpu.VMEM)
    hbm = pl.BlockSpec(memory_space=pl.ANY)
    cores, sides, hops = max(dp - 1, 1), max(mp - 1, 1), max(n - 1, 1)
    share_shape = (n * dp, LAYERS * n + -(LAYERS * n) % 8, rows + -rows % 128)

    def pair(*shape):
        return [dma(shape), dma(shape)]

    return pl.pallas_call(
        functools.partial(stack_kernel, n, dp, mp),
        out_shape=jax.ShapeDtypeStruct((rows, width), bf),
        in_specs=[vmem, vmem, vmem, vmem, vmem, hbm, hbm, hbm],
        out_specs=vmem,
        scratch_shapes=[
            pltpu.VMEM((units, full), bf),
            pltpu.VMEM((units, full), bf),
            pltpu.VMEM((units, full), bf),
            pltpu.VMEM((HALVES, mp, size, width + LANES), bf),
            pltpu.VMEM((HALVES, mp, size, width), bf),
            pltpu.VMEM((HALVES, cores, mp, n * hr, width), bf),
            pltpu.VMEM((HALVES, sides, n * hr, width), bf),
            pltpu.VMEM((HALVES, n, hr, width), bf),
            pltpu.VMEM((HALVES, n, hr, width), bf),
            pltpu.VMEM((size, units), bf),
            pltpu.VMEM((LAYERS, HALVES, size, 1), f32),
            pltpu.VMEM((2, size, 1), f32),
            pltpu.VMEM(share_shape, f32),
            dma((3,)), *pair(1),
            dma((HALVES,)), dma((HALVES, hops, PARTS)), dma((HALVES,)), dma((HALVES, hops, PARTS)),
            dma((HALVES, sides)), dma((HALVES, n, sides)), *pair(HALVES, cores),
            *pair(HALVES, mp, cores), dma((HALVES, sides)), dma((HALVES, n, PARTS, sides)),
            dma((HALVES,)), dma((HALVES, hops, PARTS)), dma((HALVES,)), dma((HALVES, hops, PARTS)),
        ],
        compiler_params=pltpu.CompilerParams(
            collective_id=0, has_side_effects=True, vmem_limit_bytes=67043328
        ),
    )(current, gain, ids, counts, exits, w_gate, w_up, w_down)


def body(hidden_in, norm_gain, expert_ids, gate_counts, exit_layer, w_gate, w_up, w_down):
    n, dp, mp = lax.axis_size("expert"), lax.axis_size("dp"), lax.axis_size("mp")
    return stack(
        n, dp, mp, hidden_in, norm_gain, expert_ids.transpose(0, 2, 1),
        gate_counts.transpose(0, 2, 1), exit_layer[None, :], w_gate, w_up, w_down,
    )


def solution(mesh):
    in_specs = (
        P(("groups", "expert", "dp"), "mp"),
        P(None, "mp"),
        P(None, ("groups", "expert", "dp"), None),
        P(None, ("groups", "expert", "dp"), None),
        P(("groups", "expert", "dp")),
        P(None, "expert", ("mp", "dp"), None),
        P(None, "expert", ("mp", "dp"), None),
        P(None, "expert", ("mp", "dp"), None),
    )
    out_specs = P(("groups", "expert", "dp"), "mp")
    return jax.shard_map(body, mesh=mesh, in_specs=in_specs, out_specs=out_specs, check_vma=False)
```

time: 146 us -> 131 us (0.90)
  Pallas kernels: 141 us -> 129 us
  other arithmetic: 2.13 us -> 0 us
    pallas_call x1, Pallas kernels: 141 us -> 129 us  [stack(): pl.pallas_call(functools.partial(stack_kernel, n, dp, mp), out_shape=jax....]
where the time goes in v2:
time: 131 us
  Pallas kernels  129 us (98%)
  local copies, waits for them, and re-layouts  1.67 us (1%)
    pallas_call x1, Pallas kernels, stack(): pl.pallas_call(functools.partial(stack_kernel, n, dp, mp), out_shape=jax....  129 us

profile of v2, /device:TPU:0, one launch (start us, length us, event | category | flops | bytes accessed | tf_op | source)
XLA Modules:
  0.0 131.0 jit_solution(6296298890519623975)
XLA Ops:
  0.0 129.3 %shard_map.82 = bf16[64,2048]{1,0:T(8,128)(2,1)} custom-call(bf16[64,2048]{1,0:T(8,128)(2,1)} %cur_ref.1, bf16[2,2048]{1,0:T(2,128)(2,1)} %gain_ref.1, s32[2,2,64]{2,1,0:T(2,128)} %bitcast.3, s32[2,2,64]{2,1,0:T(2,128)} %bitcast.4, s32[1,64]{1,0:T(1,128)} %bitcast.5, bf16[2,1,1792,4096]{3,2,1,0:T(8,128)(2,1)} %wg_hbm.1, bf16[2,1,1792,4096]{3,2,1,0:T(8,128)(2,1)} %wu_hbm.1, ...), custom_call_target="tpu_custom_call" | custom-call | tf_op jit(solution)/shard_map/pallas_call | solution.py:545
  129.3 1.7 %copy.10 = bf16[64,2048]{1,0:T(8,128)(2,1)} copy(bf16[64,2048]{1,0:T(8,128)(2,1)} %shard_map.82) | data formatting | bytes 524288

commit v3 on v2

--- a/solution.py
+++ b/solution.py
@@ -29,9 +29,9 @@
 def stack_kernel(
     n, dp, mp,
     cur_ref, gain_ref, ids_ref, counts_ref, exit_ref, wg_hbm, wu_hbm, wd_hbm, out_ref,
-    wg, wu, wd, xg, p, rd, xr, rzu, rzd, hid, col, inv, shares,
+    wg, wu, wd, xg, p, rd, xr, rzu, rzd, rzf, hid, col, inv, shares,
     w_sem, sh_s, sh_r, zu_s, zu_r, zd_s, zd_r, x_s, x_r, d_s, d_r,
-    sw_s, sw_r, bx_s, bx_r, bu_s, bu_r, bd_s, bd_r,
+    sw_s, sw_r, bx_s, bx_r, bu_s, bu_r, bd_s, bd_r, bf_s, bf_r,
 ):
     rows, width = cur_ref.shape
     full = width * mp
@@ -59,6 +59,7 @@
     place_of = {k: e + k for k in range(1 - n, n)}
     has = {k: (e + k <= n - 1 if k > 0 else e + k >= 0) for k in range(1 - n, n) if k}
     below, above = e > 0, e < n - 1
+    direct = n > 3
     up_z, down_z = {"expert": lax.rem(e + 1, n)}, {"expert": lax.rem(e + n - 1, n)}
 
     def remote(src, dst, ss, rs, dev):
@@ -292,6 +293,11 @@
         dst = rzd.at[h, blk, pl.ds(j * pr, pr)]
         return remote(src, dst, bd_s.at[h], bd_r.at[h, blk, j], down_z)
 
+    def bf(h, blk, j):
+        src = p.at[h, m, pl.ds(row_of(d, blk, j), pr)]
+        dst = rzf.at[h, pl.ds(j * pr, pr)]
+        return remote(src, dst, bf_s.at[h], bf_r.at[h, j], {"expert": n - 1 - e})
+
     def out_ref_of(h, q, first=0, count=n):
         return p.at[h, q, pl.ds(pl.multiple_of(d * core_rows + first * hr, hr), count * hr)]
 
@@ -304,11 +310,15 @@
             remote(ref, ref, bx_s.at[h, r - 1], bx_r.at[h, 0, 0, r - 1], {"mp": part(r)}).wait_send()
         for i in range(n):
             def done(i=i):
+                edge = int(direct and i in (0, n - 1))
+                if edge:
+                    ref = out_ref_of(h, m, 0, 1)
+                    remote(ref, ref, bf_s.at[h], bf_r.at[h, 0], {"expert": n - 1 - e}).wait_send()
                 if i < n - 1:
-                    ref = out_ref_of(h, m, i + 1, n - 1 - i)
+                    ref = out_ref_of(h, m, i + 1, n - 1 - i - edge)
                     remote(ref, ref, bu_s.at[h], bu_r.at[h, 0, 0], up_z).wait_send()
                 if i > 0:
-                    ref = out_ref_of(h, m, 0, i)
+                    ref = out_ref_of(h, m, edge, i - edge)
                     remote(ref, ref, bd_s.at[h], bd_r.at[h, 0, 0], down_z).wait_send()
 
             pl.when(e == i)(done)
@@ -339,13 +349,19 @@
             for r in range(1, mp):
                 bx(h, blk, j, r).wait_recv()
 
-            @pl.when(inner)
-            def _():
-                copy(h, blk, j).wait_recv()
-                joined(h, blk, j, incoming)
-
-            pl.when(jnp.logical_not(inner))(lambda: plain(h, blk, j))
-            copy(h, blk, j).start()
+            if direct and k >= n - 2:
+                plain(h, blk, j)
+            else:
+                @pl.when(inner)
+                def _():
+                    copy(h, blk, j).wait_recv()
+                    joined(h, blk, j, incoming)
+
+                pl.when(jnp.logical_not(inner))(lambda: plain(h, blk, j))
+            if direct and k == n - 1:
+                bf(h, blk, j).start()
+            else:
+                copy(h, blk, j).start()
 
         pl.when(has[k])(lambda: along(place_of[k], bu, below, rzu))
         pl.when(has[-k])(lambda: along(place_of[-k], bd, above, rzd))
@@ -356,10 +372,15 @@
                 bx(h, e, j, r).wait_recv()
             pl.when(below)(lambda j=j: bu(h, e, j).wait_recv())
             pl.when(above)(lambda j=j: bd(h, e, j).wait_recv())
-
-        def finish(sources):
+            if direct:
+                pl.when(e == 0)(lambda j=j: bf(h, e, j).wait_recv())
+                pl.when(e == n - 1)(lambda j=j: bf(h, e, j).wait_recv())
+
+        def finish(sources, far_too=False):
             def put(off):
                 _, v = gathered(h, e, off)
+                if far_too:
+                    v = v + rzf[h, pl.ds(off, CHUNK), :].astype(jnp.float32)
                 for ref in sources:
                     v = v + ref[h, e, pl.ds(off, CHUNK), :].astype(jnp.float32)
                 at = pl.ds(pl.multiple_of(h * hr + off, CHUNK), CHUNK)
@@ -370,8 +391,8 @@
         if n == 1:
             finish([])
         else:
-            pl.when(jnp.logical_not(below))(lambda: finish([rzd]))
-            pl.when(jnp.logical_not(above))(lambda: finish([rzu]))
+            pl.when(jnp.logical_not(below))(lambda: finish([rzd], direct))
+            pl.when(jnp.logical_not(above))(lambda: finish([rzu], direct))
             if n > 2:
                 pl.when(jnp.logical_and(below, above))(lambda: finish([rzu, rzd]))
 
@@ -423,6 +444,8 @@
 
     both = range(PARTS)
     far = list(range(n - 1, 0, -1))
+    if direct:
+        far[0:2] = [n - 2, n - 1]
 
     def start_own(h):
         for j in both:
@@ -449,11 +472,12 @@
             for copy in share_copies():
                 copy.start()
             own_rows(1, 0, cur_ref)
-            for j in both:
-                spread(1, j, e)
+            spread(1, 0, e)
             for s in range(1, n):
                 z_all(0, s)
                 if s == 1:
+                    for j in both[1:]:
+                        spread(1, j, e)
                     for i in range(3):
                         weight(0, i).start()
                 if s == max(n - 2, 1):
@@ -465,9 +489,9 @@
             own_rows(0, layer_idx, out_ref)
             start_own(0)
             swap_wait(1, 0)
-            for k in far:
+            for i, k in enumerate(far):
                 back_all(1, k)
-                z_all(0, n - k)
+                z_all(0, i + 1)
             arrive(1, cur_ref)
             own_rows(1, layer_idx, out_ref)
             start_own(1)
@@ -480,7 +504,7 @@
         scales(0, layer_idx)
         weight(layer_idx, 0).wait()
         weight(layer_idx, 1).wait()
-        events = [(2 * s - 2, lambda s=s: z_all(1, s)) for s in range(2, n)]
+        events = [(3 * s - 4, lambda s=s: z_all(1, s)) for s in range(2, n)]
         events += [(5, lambda s=s: x_step(1, s)) for s in range(n - 2)]
         hidden(0, layer_idx, events)
         weight(layer_idx, 2).wait()
@@ -491,8 +515,8 @@
             project(0, r)
         if n > 1:
             x_step(1, n - 2)
-        project(0, 0, [(0, lambda: back_x_all(0))])
-        x_step(1, n - 1)
+        last_x = [(0, lambda: x_step(1, n - 1))] if n > 1 else []
+        project(0, 0, [(0, lambda: back_x_all(0))] + last_x)
         core_done(1)
         scales(1, layer_idx)
         rest = [(k, j) for k in far for j in both]
@@ -557,6 +581,7 @@
             pltpu.VMEM((HALVES, sides, n * hr, width), bf),
             pltpu.VMEM((HALVES, n, hr, width), bf),
             pltpu.VMEM((HALVES, n, hr, width), bf),
+            pltpu.VMEM((HALVES, hr, width), bf),
             pltpu.VMEM((size, units), bf),
             pltpu.VMEM((LAYERS, HALVES, size, 1), f32),
             pltpu.VMEM((2, size, 1), f32),
@@ -566,6 +591,7 @@
             dma((HALVES, sides)), dma((HALVES, n, sides)), *pair(HALVES, cores),
             *pair(HALVES, mp, cores), dma((HALVES, sides)), dma((HALVES, n, PARTS, sides)),
             dma((HALVES,)), dma((HALVES, hops, PARTS)), dma((HALVES,)), dma((HALVES, hops, PARTS)),
+            dma((HALVES,)), dma((HALVES, PARTS)),
         ],
         compiler_params=pltpu.CompilerParams(
             collective_id=0, has_side_effects=True, vmem_limit_bytes=67043328

time: 131 us -> 128 us (0.977)
  Pallas kernels: 129 us -> 126 us
    pallas_call x1, Pallas kernels: 129 us -> 126 us  [stack(): pl.pallas_call(functools.partial(stack_kernel, n, dp, mp), out_shape=jax....]
where the time goes in v3:
time: 128 us
  Pallas kernels  126 us (98%)
  local copies, waits for them, and re-layouts  1.67 us (1%)
    pallas_call x1, Pallas kernels, stack(): pl.pallas_call(functools.partial(stack_kernel, n, dp, mp), out_shape=jax....  126 us

profile of v3, /device:TPU:0, one launch (start us, length us, event | category | flops | bytes accessed | tf_op | source)
XLA Modules:
  0.0 127.8 jit_solution(6012013682887149386)
XLA Ops:
  0.0 126.1 %shard_map.82 = bf16[64,2048]{1,0:T(8,128)(2,1)} custom-call(bf16[64,2048]{1,0:T(8,128)(2,1)} %cur_ref.1, bf16[2,2048]{1,0:T(2,128)(2,1)} %gain_ref.1, s32[2,2,64]{2,1,0:T(2,128)} %bitcast.3, s32[2,2,64]{2,1,0:T(2,128)} %bitcast.4, s32[1,64]{1,0:T(1,128)} %bitcast.5, bf16[2,1,1792,4096]{3,2,1,0:T(8,128)(2,1)} %wg_hbm.1, bf16[2,1,1792,4096]{3,2,1,0:T(8,128)(2,1)} %wu_hbm.1, ...), custom_call_target="tpu_custom_call" | custom-call | tf_op jit(solution)/shard_map/pallas_call | solution.py:569
  126.1 1.7 %copy.10 = bf16[64,2048]{1,0:T(8,128)(2,1)} copy(bf16[64,2048]{1,0:T(8,128)(2,1)} %shard_map.82) | data formatting | bytes 524288
